TPU v7x, 256 devices: a whole 4x4x8 slice. The times are simulated.
256 devices in a mesh: ens: 64 (over z_lo, x, y), row: 2 (over z_hi), col: 2 (over core).
Axes of the slice: x: 4, y: 4, z: 8 (z_hi: 2, z_lo: 4; z = z_hi * 4 + z_lo), core: 2. Of those that a mesh axis runs over, the one named last changes fastest.
Arguments:
- states: float32 [128, 16, 4096], P('ens', None, ('row', 'col')), parts along dimension 0, may hold values from -4 to 4
- jacobian: bfloat16 [262144, 4096], P(('ens', 'row'), 'col'), parts along dimension 0, as said below
- step_sizes: float32 [128, 1], P('ens'), parts along dimension 0, may hold values from 0.75 to 1.5
Outputs:
- new_states: float32 [128, 16, 4096], P('ens', None, ('row', 'col')), parts along dimension 0
There are 64 independent parts, one for each index of `ens`. A program takes and returns all parts, laid end to end along the dimension named above; each array names one. Nothing has to cross between parts.
Inputs may be any that keep to these rules, and one draw needn't show every extreme that they name: `jacobian`: the diagonal lies between -40 and -1 apart from a term as small as the others, whose magnitude is at most 24 / sqrt(4096).
All inputs are finite; a program needn't handle non-finite values.
Results may differ from a plain program's by a relative error of at most 0.0083.
Values may be sent and summed in bfloat16 or wider, within the bound.
No kernel may reach another device: no remote copies, remote signals or barrier semaphores. Data moves between devices by JAX's collectives and lax.ppermute only.
A program may use at most 64 MiB of HBM per device.

v0:
```python
import jax
import jax.numpy as jnp
from jax import lax
from jax.sharding import PartitionSpec as P

BLOCKS = 12
precise = lax.Precision.HIGHEST
squarings = 10
taylor_degree = 8


def cut_along(shard, dim, length):
    before, after = (shard.shape[:dim], shard.shape[dim + 1 :])
    return jnp.moveaxis(shard.reshape(*before, length, -1, *after), dim, 0)


def sum_at_owner(shard, axis, dim):
    tiles = cut_along(shard, dim, lax.axis_size(axis))
    arrived = lax.all_to_all(tiles, axis, split_axis=0, concat_axis=0, tiled=True)
    return arrived.sum(axis=0)


def total_of_pieces(shard, axis):
    return lax.all_gather(shard, axis).sum(0)


def from_everyone(shard, axis):
    copies = jnp.broadcast_to(shard, (lax.axis_size(axis), *shard.shape))
    return lax.all_to_all(copies, axis, split_axis=0, concat_axis=0, tiled=True)


def of_everyone(shard, axis):
    everything = from_everyone(shard, axis)
    return jnp.sum(everything, axis=0)


def together(arrays, axis):
    ends = [0]
    for a in arrays:
        ends.append(ends[-1] + a.size)
    subtotal = of_everyone(jnp.concatenate([a.ravel() for a in arrays]), axis)
    return tuple((subtotal[b:e].reshape(a.shape) for a, b, e in zip(arrays, ends, ends[1:])))


def exponential(matrix):
    scaled = matrix / 2.0**squarings
    identity = jnp.eye(matrix.shape[-1], dtype=jnp.float32)
    result = jnp.broadcast_to(identity, matrix.shape)
    for degree in range(taylor_degree, 0, -1):
        result = identity + jnp.matmul(scaled, result, precision=precise) / degree
    for squaring in range(squarings):
        result = jnp.matmul(result, result, precision=precise)
    return result


def apply_jacobian(vectors, jacobian):
    rounded = vectors.astype(jnp.bfloat16)
    gathered = lax.all_gather(rounded, ("row", "col"), axis=2, tiled=True)
    tile_cols = jacobian.shape[1]
    column_piece = lax.dynamic_slice_in_dim(
        gathered, lax.axis_index("col") * tile_cols, tile_cols, 2
    )
    partial_value = jnp.einsum(
        "bcm,nm->bcn", column_piece, jacobian, preferred_element_type=jnp.float32
    )
    return sum_at_owner(partial_value, "col", 2)


def sum_projections(terms):
    return total_of_pieces(terms, ("row", "col"))


def sum_grams(terms):
    return total_of_pieces(terms, ("row", "col"))


def sum_combined(terms):
    return together((terms[0], terms[1]), ("row", "col"))


def local_gram(vectors):
    return jnp.einsum("bpn,bqn->bpq", vectors, vectors, precision=precise)


def project_block(krylov_basis, images):
    local_terms = jnp.einsum("bkn,bqn->bkq", krylov_basis, images, precision=precise)
    projection, raw_gram = sum_combined((local_terms, local_gram(images)))
    reduced = images - jnp.einsum("bkq,bkn->bqn", projection, krylov_basis, precision=precise)
    gram_matrix = raw_gram - jnp.einsum("bkp,bkq->bpq", projection, projection, precision=precise)
    return (projection, reduced, gram_matrix)


def local(states, jacobian, step_sizes):
    members = states.shape[0]
    columns = states.shape[1]
    length = states.shape[2]
    krylov = BLOCKS * columns
    forcing = apply_jacobian(states, jacobian) - states * states * states / 3.0
    root_lower = jnp.linalg.cholesky(sum_grams(local_gram(forcing)))
    leading = lax.linalg.triangular_solve(root_lower, forcing, left_side=True, lower=True)
    krylov_basis = jnp.zeros((members, krylov, length), jnp.float32)
    krylov_basis = lax.dynamic_update_slice_in_dim(krylov_basis, leading, 0, 1)
    hessenberg = jnp.zeros((members, krylov, krylov), jnp.float32)

    def arnoldi_turn(block_index, carry):
        basis_now, hess_now = carry
        start = block_index * columns
        current = lax.dynamic_slice_in_dim(basis_now, start, columns, 1)
        images = apply_jacobian(current, jacobian)
        projection, reduced, gram_matrix = project_block(basis_now, images)
        lower_factor = jnp.linalg.cholesky(gram_matrix)
        next_block = lax.linalg.triangular_solve(lower_factor, reduced, left_side=True, lower=True)
        hess_now = lax.dynamic_update_slice_in_dim(hess_now, projection, start, 2)
        sub_block = jnp.swapaxes(lower_factor, 1, 2)
        hess_now = lax.dynamic_update_slice(
            hess_now, sub_block, (jnp.int32(0), start + columns, start)
        )
        basis_now = lax.dynamic_update_slice_in_dim(basis_now, next_block, start + columns, 1)
        return (basis_now, hess_now)

    krylov_basis, hessenberg = lax.fori_loop(
        0, BLOCKS - 1, arnoldi_turn, (krylov_basis, hessenberg)
    )
    last_start = (BLOCKS - 1) * columns
    last_block = krylov_basis[:, last_start : last_start + columns]
    last_images = apply_jacobian(last_block, jacobian)
    last_column = sum_projections(
        jnp.einsum("bkn,bqn->bkq", krylov_basis, last_images, precision=precise)
    )
    hessenberg = hessenberg.at[:, :, last_start : last_start + columns].set(last_column)
    step_size = step_sizes[:, 0][:, None, None]
    augmented = jnp.zeros((members, krylov + columns, krylov + columns), jnp.float32)
    augmented = augmented.at[:, :krylov, :krylov].set(step_size * hessenberg)
    augmented = augmented.at[:, :columns, krylov:].set(step_size * jnp.swapaxes(root_lower, 1, 2))
    exponent = exponential(augmented)
    phi_block = exponent[:, :krylov, krylov:]
    states = states + jnp.einsum("bkq,bkn->bqn", phi_block, krylov_basis, precision=precise)
    return states


def solution(mesh):
    placed = (P("ens", None, ("row", "col")), P(("ens", "row"), "col"), P("ens", None))
    return jax.shard_map(
        local, mesh=mesh, in_specs=placed, out_specs=P("ens", None, ("row", "col")), check_vma=False
    )
```

profile of v0, /device:TPU:1, one launch (start us, length us, event | category | flops | bytes accessed | tf_op | source)
XLA Modules:
  0.0 581.9 jit_solution(12738345656807627171)
XLA Ops:
  0.9 12.9 %all_gather.28 = bf16[2,16,4096]{2,1,0:T(8,128)(2,1)S(1)} all-gather(bf16[2,16,1024]{2,1,0:T(8,128)(2,1)S(1)} %convert_element_type.38), channel_id=1, replica_groups=mesh['ens'=64,'row'=2,'col'=2] {'row','col'}, dimensions={2}, use_global_device_ids=true | all-gather | bytes 327680 | tf_op jit(solution)/shard_map/all_gather | solution.py:58
  13.8 6.0 %fusion.9 = f32[2,16,2048]{2,1,0:T(8,128)S(1)} fusion(bf16[2048,2048]{1,0:T(8,128)(2,1)} %param.15, bf16[2,16,4096]{2,1,0:T(8,128)(2,1)S(1)} %all_gather.28, s32[]{:T(128)S(6)} %select_n.40), kind=kOutput, calls=%fused_computation.24 | convolution fusion | flops 268435456 | bytes 8781828 | tf_op jit(solution)/shard_map/bcm,nm->bcn/dot_general | solution.py:63
  19.8 3.7 all_to_all.37
  23.9 9.3 %all-gather = f32[8,16,16]{2,1,0:T(8,128)S(1)} all-gather(f32[2,16,16]{2,1,0:T(8,128)S(1)} %fusion.45), channel_id=2, replica_groups=mesh['ens'=64,'row'=2,'col'=2] {'row','col'}, dimensions={0}, use_global_device_ids=true | all-gather | bytes 10240 | tf_op jit(solution)/shard_map/all_gather | solution.py:24
  39.6 487.2 %while.20 = (s32[]{:T(128)}, f32[2,192,1024]{2,1,0:T(8,128)S(1)}, f32[2,192,192]{1,2,0:T(8,128)S(1)}, bf16[2048,2048]{1,0:T(8,128)(2,1)}, s32[]{:T(128)}, /*inde...) while((s32[]{:T(128)}, f32[2,192,1024]{2,1,0:T(8,128)S(1)}, ...), condition=%wide.region_7.10_spmd, body=%wide.region_4.9_spmd.sunk | while | flops 433289760 | bytes 15701595 | solution.py:121
  39.6 9.9 %all_gather.35 = bf16[2,16,4096]{2,1,0:T(8,128)(2,1)S(1)} all-gather(bf16[2,16,1024]{2,1,0:T(8,128)(2,1)S(1)} %dynamic-slice_convert_fusion.2), channel_id=1, replica_groups=mesh['ens'=64,'row'=2,'col'=2] {'row','col'}, dimensions={2}, use_global_device_ids=true | all-gather | bytes 327680 | tf_op jit(solution)/shard_map/while/body/eval_jaxpr/all_gather | solution.py:58
  49.5 6.0 %fusion.139 = f32[2,16,2048]{2,1,0:T(8,128)S(1)} fusion(bf16[2048,2048]{1,0:T(8,128)(2,1)} %get-tuple-element.226, bf16[2,16,4096]{2,1,0:T(8,128)(2,1)S(1)} %all_gather.35, s32[]{:T(128)S(6)} %select_n.61), kind=kOutput, calls=%fused_computation.clone.1 | convolution fusion | flops 268435456 | bytes 8781828 | tf_op jit(solution)/shard_map/while/body/eval_jaxpr/bcm,nm->bcn/dot_general | solution.py:63
  62.0 7.1 %all-to-all-start.1 = ((f32[4,1,6656]{2,1,0:T(1,128)}), f32[4,1,6656]{2,1,0:T(1,128)S(1)}, u32[]{:S(2)}, u32[]{:S(2)}) async-start(f32[4,1,6656]{2,1,0:T(1,128)} %broadcast_in_dim.16), calls=%async_computation.1 | async-start | bytes 212992 | tf_op jit(solution)/shard_map/while/body/eval_jaxpr/all_to_all | solution.py:29
  69.0 7.3 %all-to-all-done.1 = f32[4,1,6656]{2,1,0:T(1,128)S(1)} async-done(((f32[4,1,6656]{2,1,0:T(1,128)}), f32[4,1,6656]{2,1,0:T(1,128)S(1)}, u32[]{:S(2)}, u32[]{:S(2)}) %all-to-all-start.1) | async-done | bytes 106528 | tf_op jit(solution)/shard_map/while/body/eval_jaxpr/all_to_all | solution.py:29
  85.5 10.6 %all_gather.35 = bf16[2,16,4096]{2,1,0:T(8,128)(2,1)S(1)} all-gather(bf16[2,16,1024]{2,1,0:T(8,128)(2,1)S(1)} %dynamic-slice_convert_fusion.2), channel_id=1, replica_groups=mesh['ens'=64,'row'=2,'col'=2] {'row','col'}, dimensions={2}, use_global_device_ids=true | all-gather | bytes 327680 | tf_op jit(solution)/shard_map/while/body/eval_jaxpr/all_gather | solution.py:58
  96.1 6.0 %fusion.139 = f32[2,16,2048]{2,1,0:T(8,128)S(1)} fusion(bf16[2048,2048]{1,0:T(8,128)(2,1)} %get-tuple-element.226, bf16[2,16,4096]{2,1,0:T(8,128)(2,1)S(1)} %all_gather.35, s32[]{:T(128)S(6)} %select_n.61), kind=kOutput, calls=%fused_computation.clone.1 | convolution fusion | flops 268435456 | bytes 8781828 | tf_op jit(solution)/shard_map/while/body/eval_jaxpr/bcm,nm->bcn/dot_general | solution.py:63
  102.1 3.7 all_to_all.38
  112.2 7.3 %all-to-all-done.1 = f32[4,1,6656]{2,1,0:T(1,128)S(1)} async-done(((f32[4,1,6656]{2,1,0:T(1,128)}), f32[4,1,6656]{2,1,0:T(1,128)S(1)}, u32[]{:S(2)}, u32[]{:S(2)}) %all-to-all-start.1) | async-done | bytes 106528 | tf_op jit(solution)/shard_map/while/body/eval_jaxpr/all_to_all | solution.py:29
  128.7 11.8 %all_gather.35 = bf16[2,16,4096]{2,1,0:T(8,128)(2,1)S(1)} all-gather(bf16[2,16,1024]{2,1,0:T(8,128)(2,1)S(1)} %dynamic-slice_convert_fusion.2), channel_id=1, replica_groups=mesh['ens'=64,'row'=2,'col'=2] {'row','col'}, dimensions={2}, use_global_device_ids=true | all-gather | bytes 327680 | tf_op jit(solution)/shard_map/while/body/eval_jaxpr/all_gather | solution.py:58
  140.5 6.0 %fusion.139 = f32[2,16,2048]{2,1,0:T(8,128)S(1)} fusion(bf16[2048,2048]{1,0:T(8,128)(2,1)} %get-tuple-element.226, bf16[2,16,4096]{2,1,0:T(8,128)(2,1)S(1)} %all_gather.35, s32[]{:T(128)S(6)} %select_n.61), kind=kOutput, calls=%fused_computation.clone.1 | convolution fusion | flops 268435456 | bytes 8781828 | tf_op jit(solution)/shard_map/while/body/eval_jaxpr/bcm,nm->bcn/dot_general | solution.py:63
  146.5 3.7 all_to_all.38
  156.7 7.4 %all-to-all-done.1 = f32[4,1,6656]{2,1,0:T(1,128)S(1)} async-done(((f32[4,1,6656]{2,1,0:T(1,128)}), f32[4,1,6656]{2,1,0:T(1,128)S(1)}, u32[]{:S(2)}, u32[]{:S(2)}) %all-to-all-start.1) | async-done | bytes 106528 | tf_op jit(solution)/shard_map/while/body/eval_jaxpr/all_to_all | solution.py:29
  173.2 11.6 %all_gather.35 = bf16[2,16,4096]{2,1,0:T(8,128)(2,1)S(1)} all-gather(bf16[2,16,1024]{2,1,0:T(8,128)(2,1)S(1)} %dynamic-slice_convert_fusion.2), channel_id=1, replica_groups=mesh['ens'=64,'row'=2,'col'=2] {'row','col'}, dimensions={2}, use_global_device_ids=true | all-gather | bytes 327680 | tf_op jit(solution)/shard_map/while/body/eval_jaxpr/all_gather | solution.py:58
  184.9 6.0 %fusion.139 = f32[2,16,2048]{2,1,0:T(8,128)S(1)} fusion(bf16[2048,2048]{1,0:T(8,128)(2,1)} %get-tuple-element.226, bf16[2,16,4096]{2,1,0:T(8,128)(2,1)S(1)} %all_gather.35, s32[]{:T(128)S(6)} %select_n.61), kind=kOutput, calls=%fused_computation.clone.1 | convolution fusion | flops 268435456 | bytes 8781828 | tf_op jit(solution)/shard_map/while/body/eval_jaxpr/bcm,nm->bcn/dot_general | solution.py:63
  190.9 3.7 all_to_all.38
  201.0 7.4 %all-to-all-done.1 = f32[4,1,6656]{2,1,0:T(1,128)S(1)} async-done(((f32[4,1,6656]{2,1,0:T(1,128)}), f32[4,1,6656]{2,1,0:T(1,128)S(1)}, u32[]{:S(2)}, u32[]{:S(2)}) %all-to-all-start.1) | async-done | bytes 106528 | tf_op jit(solution)/shard_map/while/body/eval_jaxpr/all_to_all | solution.py:29
  217.6 11.6 %all_gather.35 = bf16[2,16,4096]{2,1,0:T(8,128)(2,1)S(1)} all-gather(bf16[2,16,1024]{2,1,0:T(8,128)(2,1)S(1)} %dynamic-slice_convert_fusion.2), channel_id=1, replica_groups=mesh['ens'=64,'row'=2,'col'=2] {'row','col'}, dimensions={2}, use_global_device_ids=true | all-gather | bytes 327680 | tf_op jit(solution)/shard_map/while/body/eval_jaxpr/all_gather | solution.py:58
  229.2 6.0 %fusion.139 = f32[2,16,2048]{2,1,0:T(8,128)S(1)} fusion(bf16[2048,2048]{1,0:T(8,128)(2,1)} %get-tuple-element.226, bf16[2,16,4096]{2,1,0:T(8,128)(2,1)S(1)} %all_gather.35, s32[]{:T(128)S(6)} %select_n.61), kind=kOutput, calls=%fused_computation.clone.1 | convolution fusion | flops 268435456 | bytes 8781828 | tf_op jit(solution)/shard_map/while/body/eval_jaxpr/bcm,nm->bcn/dot_general | solution.py:63
  245.4 7.4 %all-to-all-done.1 = f32[4,1,6656]{2,1,0:T(1,128)S(1)} async-done(((f32[4,1,6656]{2,1,0:T(1,128)}), f32[4,1,6656]{2,1,0:T(1,128)S(1)}, u32[]{:S(2)}, u32[]{:S(2)}) %all-to-all-start.1) | async-done | bytes 106528 | tf_op jit(solution)/shard_map/while/body/eval_jaxpr/all_to_all | solution.py:29
  261.9 11.6 %all_gather.35 = bf16[2,16,4096]{2,1,0:T(8,128)(2,1)S(1)} all-gather(bf16[2,16,1024]{2,1,0:T(8,128)(2,1)S(1)} %dynamic-slice_convert_fusion.2), channel_id=1, replica_groups=mesh['ens'=64,'row'=2,'col'=2] {'row','col'}, dimensions={2}, use_global_device_ids=true | all-gather | bytes 327680 | tf_op jit(solution)/shard_map/while/body/eval_jaxpr/all_gather | solution.py:58
  273.6 6.0 %fusion.139 = f32[2,16,2048]{2,1,0:T(8,128)S(1)} fusion(bf16[2048,2048]{1,0:T(8,128)(2,1)} %get-tuple-element.226, bf16[2,16,4096]{2,1,0:T(8,128)(2,1)S(1)} %all_gather.35, s32[]{:T(128)S(6)} %select_n.61), kind=kOutput, calls=%fused_computation.clone.1 | convolution fusion | flops 268435456 | bytes 8781828 | tf_op jit(solution)/shard_map/while/body/eval_jaxpr/bcm,nm->bcn/dot_general | solution.py:63
  279.6 3.7 all_to_all.38
  289.7 7.4 %all-to-all-done.1 = f32[4,1,6656]{2,1,0:T(1,128)S(1)} async-done(((f32[4,1,6656]{2,1,0:T(1,128)}), f32[4,1,6656]{2,1,0:T(1,128)S(1)}, u32[]{:S(2)}, u32[]{:S(2)}) %all-to-all-start.1) | async-done | bytes 106528 | tf_op jit(solution)/shard_map/while/body/eval_jaxpr/all_to_all | solution.py:29
  306.3 11.6 %all_gather.35 = bf16[2,16,4096]{2,1,0:T(8,128)(2,1)S(1)} all-gather(bf16[2,16,1024]{2,1,0:T(8,128)(2,1)S(1)} %dynamic-slice_convert_fusion.2), channel_id=1, replica_groups=mesh['ens'=64,'row'=2,'col'=2] {'row','col'}, dimensions={2}, use_global_device_ids=true | all-gather | bytes 327680 | tf_op jit(solution)/shard_map/while/body/eval_jaxpr/all_gather | solution.py:58
  317.9 6.0 %fusion.139 = f32[2,16,2048]{2,1,0:T(8,128)S(1)} fusion(bf16[2048,2048]{1,0:T(8,128)(2,1)} %get-tuple-element.226, bf16[2,16,4096]{2,1,0:T(8,128)(2,1)S(1)} %all_gather.35, s32[]{:T(128)S(6)} %select_n.61), kind=kOutput, calls=%fused_computation.clone.1 | convolution fusion | flops 268435456 | bytes 8781828 | tf_op jit(solution)/shard_map/while/body/eval_jaxpr/bcm,nm->bcn/dot_general | solution.py:63
  323.9 3.7 all_to_all.38
  334.0 7.4 %all-to-all-done.1 = f32[4,1,6656]{2,1,0:T(1,128)S(1)} async-done(((f32[4,1,6656]{2,1,0:T(1,128)}), f32[4,1,6656]{2,1,0:T(1,128)S(1)}, u32[]{:S(2)}, u32[]{:S(2)}) %all-to-all-start.1) | async-done | bytes 106528 | tf_op jit(solution)/shard_map/while/body/eval_jaxpr/all_to_all | solution.py:29
  350.6 11.6 %all_gather.35 = bf16[2,16,4096]{2,1,0:T(8,128)(2,1)S(1)} all-gather(bf16[2,16,1024]{2,1,0:T(8,128)(2,1)S(1)} %dynamic-slice_convert_fusion.2), channel_id=1, replica_groups=mesh['ens'=64,'row'=2,'col'=2] {'row','col'}, dimensions={2}, use_global_device_ids=true | all-gather | bytes 327680 | tf_op jit(solution)/shard_map/while/body/eval_jaxpr/all_gather | solution.py:58
  362.2 6.0 %fusion.139 = f32[2,16,2048]{2,1,0:T(8,128)S(1)} fusion(bf16[2048,2048]{1,0:T(8,128)(2,1)} %get-tuple-element.226, bf16[2,16,4096]{2,1,0:T(8,128)(2,1)S(1)} %all_gather.35, s32[]{:T(128)S(6)} %select_n.61), kind=kOutput, calls=%fused_computation.clone.1 | convolution fusion | flops 268435456 | bytes 8781828 | tf_op jit(solution)/shard_map/while/body/eval_jaxpr/bcm,nm->bcn/dot_general | solution.py:63
  378.4 7.4 %all-to-all-done.1 = f32[4,1,6656]{2,1,0:T(1,128)S(1)} async-done(((f32[4,1,6656]{2,1,0:T(1,128)}), f32[4,1,6656]{2,1,0:T(1,128)S(1)}, u32[]{:S(2)}, u32[]{:S(2)}) %all-to-all-start.1) | async-done | bytes 106528 | tf_op jit(solution)/shard_map/while/body/eval_jaxpr/all_to_all | solution.py:29
  394.3 11.6 %all_gather.35 = bf16[2,16,4096]{2,1,0:T(8,128)(2,1)S(1)} all-gather(bf16[2,16,1024]{2,1,0:T(8,128)(2,1)S(1)} %dynamic-slice_convert_fusion.2), channel_id=1, replica_groups=mesh['ens'=64,'row'=2,'col'=2] {'row','col'}, dimensions={2}, use_global_device_ids=true | all-gather | bytes 327680 | tf_op jit(solution)/shard_map/while/body/eval_jaxpr/all_gather | solution.py:58
  405.9 6.0 %fusion.139 = f32[2,16,2048]{2,1,0:T(8,128)S(1)} fusion(bf16[2048,2048]{1,0:T(8,128)(2,1)} %get-tuple-element.226, bf16[2,16,4096]{2,1,0:T(8,128)(2,1)S(1)} %all_gather.35, s32[]{:T(128)S(6)} %select_n.61), kind=kOutput, calls=%fused_computation.clone.1 | convolution fusion | flops 268435456 | bytes 8781828 | tf_op jit(solution)/shard_map/while/body/eval_jaxpr/bcm,nm->bcn/dot_general | solution.py:63
  422.0 7.4 %all-to-all-done.1 = f32[4,1,6656]{2,1,0:T(1,128)S(1)} async-done(((f32[4,1,6656]{2,1,0:T(1,128)}), f32[4,1,6656]{2,1,0:T(1,128)S(1)}, u32[]{:S(2)}, u32[]{:S(2)}) %all-to-all-start.1) | async-done | bytes 106528 | tf_op jit(solution)/shard_map/while/body/eval_jaxpr/all_to_all | solution.py:29
  438.4 11.6 %all_gather.35 = bf16[2,16,4096]{2,1,0:T(8,128)(2,1)S(1)} all-gather(bf16[2,16,1024]{2,1,0:T(8,128)(2,1)S(1)} %dynamic-slice_convert_fusion.2), channel_id=1, replica_groups=mesh['ens'=64,'row'=2,'col'=2] {'row','col'}, dimensions={2}, use_global_device_ids=true | all-gather | bytes 327680 | tf_op jit(solution)/shard_map/while/body/eval_jaxpr/all_gather | solution.py:58
  450.1 6.0 %fusion.139 = f32[2,16,2048]{2,1,0:T(8,128)S(1)} fusion(bf16[2048,2048]{1,0:T(8,128)(2,1)} %get-tuple-element.226, bf16[2,16,4096]{2,1,0:T(8,128)(2,1)S(1)} %all_gather.35, s32[]{:T(128)S(6)} %select_n.61), kind=kOutput, calls=%fused_computation.clone.1 | convolution fusion | flops 268435456 | bytes 8781828 | tf_op jit(solution)/shard_map/while/body/eval_jaxpr/bcm,nm->bcn/dot_general | solution.py:63
  466.2 7.4 %all-to-all-done.1 = f32[4,1,6656]{2,1,0:T(1,128)S(1)} async-done(((f32[4,1,6656]{2,1,0:T(1,128)}), f32[4,1,6656]{2,1,0:T(1,128)S(1)}, u32[]{:S(2)}, u32[]{:S(2)}) %all-to-all-start.1) | async-done | bytes 106528 | tf_op jit(solution)/shard_map/while/body/eval_jaxpr/all_to_all | solution.py:29
  482.6 11.6 %all_gather.35 = bf16[2,16,4096]{2,1,0:T(8,128)(2,1)S(1)} all-gather(bf16[2,16,1024]{2,1,0:T(8,128)(2,1)S(1)} %dynamic-slice_convert_fusion.2), channel_id=1, replica_groups=mesh['ens'=64,'row'=2,'col'=2] {'row','col'}, dimensions={2}, use_global_device_ids=true | all-gather | bytes 327680 | tf_op jit(solution)/shard_map/while/body/eval_jaxpr/all_gather | solution.py:58
  494.3 6.0 %fusion.139 = f32[2,16,2048]{2,1,0:T(8,128)S(1)} fusion(bf16[2048,2048]{1,0:T(8,128)(2,1)} %get-tuple-element.226, bf16[2,16,4096]{2,1,0:T(8,128)(2,1)S(1)} %all_gather.35, s32[]{:T(128)S(6)} %select_n.61), kind=kOutput, calls=%fused_computation.clone.1 | convolution fusion | flops 268435456 | bytes 8781828 | tf_op jit(solution)/shard_map/while/body/eval_jaxpr/bcm,nm->bcn/dot_general | solution.py:63
  500.3 3.7 all_to_all.38
  510.4 7.4 %all-to-all-done.1 = f32[4,1,6656]{2,1,0:T(1,128)S(1)} async-done(((f32[4,1,6656]{2,1,0:T(1,128)}), f32[4,1,6656]{2,1,0:T(1,128)S(1)}, u32[]{:S(2)}, u32[]{:S(2)}) %all-to-all-start.1) | async-done | bytes 106528 | tf_op jit(solution)/shard_map/while/body/eval_jaxpr/all_to_all | solution.py:29
  526.8 11.8 %all_gather.31 = bf16[2,16,4096]{2,1,0:T(8,128)(2,1)S(1)} all-gather(bf16[2,16,1024]{2,1,0:T(8,128)(2,1)S(1)} %slice.135), channel_id=1, replica_groups=mesh['ens'=64,'row'=2,'col'=2] {'row','col'}, dimensions={2}, use_global_device_ids=true | all-gather | bytes 327680 | tf_op jit(solution)/shard_map/all_gather | solution.py:58
  538.6 6.0 %fusion.7 = f32[2,16,2048]{2,1,0:T(8,128)S(1)} fusion(bf16[2048,2048]{1,0:T(8,128)(2,1)} %get-tuple-element.236, bf16[2,16,4096]{2,1,0:T(8,128)(2,1)S(1)} %all_gather.31, s32[]{:T(128)S(6)} %select_n.40), kind=kOutput, calls=%fused_computation.22 | convolution fusion | flops 268435456 | bytes 8781828 | tf_op jit(solution)/shard_map/bcm,nm->bcn/dot_general | solution.py:63
  551.7 9.6 %all-gather.1 = f32[8,192,16]{1,2,0:T(8,128)S(1)} all-gather(f32[2,192,16]{1,2,0:T(8,128)S(1)} %fusion.63), channel_id=3, replica_groups=mesh['ens'=64,'row'=2,'col'=2] {'row','col'}, dimensions={0}, use_global_device_ids=true | all-gather | bytes 122880 | tf_op jit(solution)/shard_map/all_gather | solution.py:24
  (414 shorter events, 219.6 us)
Async XLA Ops:
  13.8 9.8 %copy-start = (f32[2,16,1024]{2,1,0:T(8,128)S(1)}, f32[2,16,1024]{2,1,0:T(8,128)}, u32[]{:S(2)}) copy-start(f32[2,16,1024]{2,1,0:T(8,128)} %param.14) | copy-start | bytes 393220
  62.0 14.3 %all-to-all-start.1 = ((f32[4,1,6656]{2,1,0:T(1,128)}), f32[4,1,6656]{2,1,0:T(1,128)S(1)}, u32[]{:S(2)}, u32[]{:S(2)}) async-start(f32[4,1,6656]{2,1,0:T(1,128)} %broadcast_in_dim.16), calls=%async_computation.1 | async-start | bytes 212992 | tf_op jit(solution)/shard_map/while/body/eval_jaxpr/all_to_all | solution.py:29
  108.6 10.9 %all-to-all-start.1 = ((f32[4,1,6656]{2,1,0:T(1,128)}), f32[4,1,6656]{2,1,0:T(1,128)S(1)}, u32[]{:S(2)}, u32[]{:S(2)}) async-start(f32[4,1,6656]{2,1,0:T(1,128)} %broadcast_in_dim.16), calls=%async_computation.1 | async-start | bytes 212992 | tf_op jit(solution)/shard_map/while/body/eval_jaxpr/all_to_all | solution.py:29
  153.0 11.0 %all-to-all-start.1 = ((f32[4,1,6656]{2,1,0:T(1,128)}), f32[4,1,6656]{2,1,0:T(1,128)S(1)}, u32[]{:S(2)}, u32[]{:S(2)}) async-start(f32[4,1,6656]{2,1,0:T(1,128)} %broadcast_in_dim.16), calls=%async_computation.1 | async-start | bytes 212992 | tf_op jit(solution)/shard_map/while/body/eval_jaxpr/all_to_all | solution.py:29
  197.4 11.0 %all-to-all-start.1 = ((f32[4,1,6656]{2,1,0:T(1,128)}), f32[4,1,6656]{2,1,0:T(1,128)S(1)}, u32[]{:S(2)}, u32[]{:S(2)}) async-start(f32[4,1,6656]{2,1,0:T(1,128)} %broadcast_in_dim.16), calls=%async_computation.1 | async-start | bytes 212992 | tf_op jit(solution)/shard_map/while/body/eval_jaxpr/all_to_all | solution.py:29
  241.7 11.0 %all-to-all-start.1 = ((f32[4,1,6656]{2,1,0:T(1,128)}), f32[4,1,6656]{2,1,0:T(1,128)S(1)}, u32[]{:S(2)}, u32[]{:S(2)}) async-start(f32[4,1,6656]{2,1,0:T(1,128)} %broadcast_in_dim.16), calls=%async_computation.1 | async-start | bytes 212992 | tf_op jit(solution)/shard_map/while/body/eval_jaxpr/all_to_all | solution.py:29
  286.0 11.0 %all-to-all-start.1 = ((f32[4,1,6656]{2,1,0:T(1,128)}), f32[4,1,6656]{2,1,0:T(1,128)S(1)}, u32[]{:S(2)}, u32[]{:S(2)}) async-start(f32[4,1,6656]{2,1,0:T(1,128)} %broadcast_in_dim.16), calls=%async_computation.1 | async-start | bytes 212992 | tf_op jit(solution)/shard_map/while/body/eval_jaxpr/all_to_all | solution.py:29
  330.4 11.0 %all-to-all-start.1 = ((f32[4,1,6656]{2,1,0:T(1,128)}), f32[4,1,6656]{2,1,0:T(1,128)S(1)}, u32[]{:S(2)}, u32[]{:S(2)}) async-start(f32[4,1,6656]{2,1,0:T(1,128)} %broadcast_in_dim.16), calls=%async_computation.1 | async-start | bytes 212992 | tf_op jit(solution)/shard_map/while/body/eval_jaxpr/all_to_all | solution.py:29
  374.7 11.0 %all-to-all-start.1 = ((f32[4,1,6656]{2,1,0:T(1,128)}), f32[4,1,6656]{2,1,0:T(1,128)S(1)}, u32[]{:S(2)}, u32[]{:S(2)}) async-start(f32[4,1,6656]{2,1,0:T(1,128)} %broadcast_in_dim.16), calls=%async_computation.1 | async-start | bytes 212992 | tf_op jit(solution)/shard_map/while/body/eval_jaxpr/all_to_all | solution.py:29
  418.4 11.0 %all-to-all-start.1 = ((f32[4,1,6656]{2,1,0:T(1,128)}), f32[4,1,6656]{2,1,0:T(1,128)S(1)}, u32[]{:S(2)}, u32[]{:S(2)}) async-start(f32[4,1,6656]{2,1,0:T(1,128)} %broadcast_in_dim.16), calls=%async_computation.1 | async-start | bytes 212992 | tf_op jit(solution)/shard_map/while/body/eval_jaxpr/all_to_all | solution.py:29
  462.6 11.0 %all-to-all-start.1 = ((f32[4,1,6656]{2,1,0:T(1,128)}), f32[4,1,6656]{2,1,0:T(1,128)S(1)}, u32[]{:S(2)}, u32[]{:S(2)}) async-start(f32[4,1,6656]{2,1,0:T(1,128)} %broadcast_in_dim.16), calls=%async_computation.1 | async-start | bytes 212992 | tf_op jit(solution)/shard_map/while/body/eval_jaxpr/all_to_all | solution.py:29
  506.8 11.0 %all-to-all-start.1 = ((f32[4,1,6656]{2,1,0:T(1,128)}), f32[4,1,6656]{2,1,0:T(1,128)S(1)}, u32[]{:S(2)}, u32[]{:S(2)}) async-start(f32[4,1,6656]{2,1,0:T(1,128)} %broadcast_in_dim.16), calls=%async_computation.1 | async-start | bytes 212992 | tf_op jit(solution)/shard_map/while/body/eval_jaxpr/all_to_all | solution.py:29
  545.3 16.6 %copy-start.1 = (f32[2,1]{0,1:T(1,128)S(1)}, f32[2,1]{0,1:T(1,128)}, u32[]{:S(2)}) copy-start(f32[2,1]{0,1:T(1,128)} %param.16) | copy-start | bytes 28
  545.3 4.9 all-to-all-start.3
  550.2 11.8 %copy-start.2 = (s32[3]{0:T(128)S(1)}, s32[3]{0:T(128)}, u32[]{:S(2)}) copy-start(s32[3]{0:T(128)} %constant.233.clone.1) | copy-start | bytes 40
where the time goes:
time: 584 us; the launch traced here: 582 us
  blocking collectives  214 us (37%)
  matrix products  131 us (22%)
  waiting for transfers between devices  82.1 us (14%)
  other arithmetic  72.9 us (12%)
  starting transfers between devices  47.2 us (8%)
  local copies, waits for them, and re-layouts  32.8 us (6%)
    all_gather x13, blocking collectives, apply_jacobian(): gathered = lax.all_gather(rounded, ('row', 'col'), axis=2, tiled=True)  150 us
    all_to_all x11, waiting for transfers between devices, from_everyone(): return lax.all_to_all(copies, axis, split_axis=0, concat_axis=0, tiled=True)  80.9 us
    dot_general x13, matrix products, apply_jacobian(): jnp.einsum('bcm,nm->bcn', column_piece, jacobian, preferred_element_type=...  77.5 us
    all_to_all x12, blocking collectives, sum_at_owner(): lax.all_to_all(tiles, axis, split_axis=0, concat_axis=0, tiled=True)  44.9 us
    all_to_all x11, starting transfers between devices, from_everyone(): return lax.all_to_all(copies, axis, split_axis=0, concat_axis=0, tiled=True)  43.5 us
    another operation x44, other arithmetic, arnoldi_turn(): lower_factor = jnp.linalg.cholesky(gram_matrix)  34 us
    another operation x22, other arithmetic, arnoldi_turn(): lax.linalg.triangular_solve(lower_factor, reduced, left_side=True, lower=...  27.2 us
    all_gather x2, blocking collectives, total_of_pieces(): return lax.all_gather(shard, axis).sum(0)  18.9 us
  transfers between devices with their start and end apart: 12, of which 12 were waited for; matrix products, arithmetic and copies ran while one was open for 0% of the time, Pallas kernels for 0%

commit v1 on v0

--- a/solution.py
+++ b/solution.py
@@ -55,7 +55,8 @@
 
 def apply_jacobian(vectors, jacobian):
     rounded = vectors.astype(jnp.bfloat16)
-    gathered = lax.all_gather(rounded, ("row", "col"), axis=2, tiled=True)
+    outgoing = jnp.stack([rounded] * lax.axis_size(("row", "col")))
+    gathered = jnp.concatenate(lax.all_to_all(outgoing, ("row", "col"), 0, 0), axis=2)
     tile_cols = jacobian.shape[1]
     column_piece = lax.dynamic_slice_in_dim(
         gathered, lax.axis_index("col") * tile_cols, tile_cols, 2

time: 584 us -> 661 us (1.13)
  waiting for transfers between devices: 82.1 us -> 197 us
  blocking collectives: 214 us -> 111 us
  starting transfers between devices: 47.2 us -> 101 us
  local copies, waits for them, and re-layouts: 32.8 us -> 41.6 us
    all_gather x13 -> x0, blocking collectives: 150 us -> none  [apply_jacobian(): gathered = lax.all_gather(rounded, ('row', 'col'), axis=2, tiled=True)]
    all_to_all x1 -> x13, waiting for transfers between devices: 1.18 us -> 116 us  [apply_jacobian(): lax.all_to_all(outgoing, ('row', 'col'), 0, 0)]
    all_to_all x1 -> x13, starting transfers between devices: 3.73 us -> 61.3 us  [apply_jacobian(): lax.all_to_all(outgoing, ('row', 'col'), 0, 0)]
    all_to_all x12 -> x13, blocking collectives: 44.9 us -> 92 us  [sum_at_owner(): lax.all_to_all(tiles, axis, split_axis=0, concat_axis=0, tiled=True)]
    another operation x1 -> x14, local copies, waits for them, and re-layouts: 0.59 us -> 9.94 us  [the longest x13 9.35 us: apply_jacobian(): outgoing = jnp.stack([rounded] * lax.axis_size(('row', 'col')))]
  transfers between devices with their start and end apart: 12 -> 24, of which waited for: 12 -> 24; matrix products, arithmetic and copies ran while one was open for 0% -> 0% of each run, Pallas kernels for 0% -> 0%
where the time goes in v1:
time: 661 us; the launch traced here: 658 us
  waiting for transfers between devices  197 us (30%)
  matrix products  132 us (20%)
  blocking collectives  111 us (17%)
  starting transfers between devices  101 us (15%)
  other arithmetic  72.9 us (11%)
  local copies, waits for them, and re-layouts  41.6 us (6%)
    all_to_all x13, waiting for transfers between devices, apply_jacobian(): lax.all_to_all(outgoing, ('row', 'col'), 0, 0)  116 us
    all_to_all x13, blocking collectives, sum_at_owner(): lax.all_to_all(tiles, axis, split_axis=0, concat_axis=0, tiled=True)  92 us
    all_to_all x11, waiting for transfers between devices, from_everyone(): return lax.all_to_all(copies, axis, split_axis=0, concat_axis=0, tiled=True)  81 us
    dot_general x13, matrix products, apply_jacobian(): jnp.einsum('bcm,nm->bcn', column_piece, jacobian, preferred_element_type=...  77.6 us
    all_to_all x13, starting transfers between devices, apply_jacobian(): lax.all_to_all(outgoing, ('row', 'col'), 0, 0)  61.3 us
    all_to_all x11, starting transfers between devices, from_everyone(): return lax.all_to_all(copies, axis, split_axis=0, concat_axis=0, tiled=True)  40 us
    another operation x44, other arithmetic, arnoldi_turn(): lower_factor = jnp.linalg.cholesky(gram_matrix)  34 us
    another operation x22, other arithmetic, arnoldi_turn(): lax.linalg.triangular_solve(lower_factor, reduced, left_side=True, lower=...  27.2 us
  transfers between devices with their start and end apart: 24, of which 24 were waited for; matrix products, arithmetic and copies ran while one was open for 0% of the time, Pallas kernels for 0%

profile of v1, /device:TPU:1, one launch (start us, length us, event | category | flops | bytes accessed | tf_op | source)
XLA Modules:
  0.0 657.5 jit_solution(11474658649161881134)
XLA Ops:
  1.6 9.9 %all-to-all-start.3 = ((bf16[4,2,16,1024]{3,2,1,0:T(8,128)(2,1)}), bf16[4,2,16,1024]{3,2,1,0:T(8,128)(2,1)S(1)}, u32[]{:S(2)}, u32[]{:S(2)}) async-start(bf16[4,2,16,1024]{3,2,1,0:T(8,128)(2,1)} %stack.15), calls=%async_computation.3 | async-start | bytes 524288 | tf_op jit(solution)/shard_map/all_to_all | solution.py:59
  11.6 8.9 %all-to-all-done.3 = bf16[4,2,16,1024]{3,2,1,0:T(8,128)(2,1)S(1)} async-done(((bf16[4,2,16,1024]{3,2,1,0:T(8,128)(2,1)}), bf16[4,2,16,1024]{3,2,1,0:T(8,128)(2,1)S(1)}, u32[]{:S(2)}, u32[]{:S(2)}) %all-to-all-start.3) | async-done | bytes 262176 | tf_op jit(solution)/shard_map/all_to_all | solution.py:59
  20.6 6.0 fusion.9
  31.6 9.3 %all-gather = f32[8,16,16]{2,1,0:T(8,128)S(1)} all-gather(f32[2,16,16]{2,1,0:T(8,128)S(1)} %fusion.45), channel_id=2, replica_groups=mesh['ens'=64,'row'=2,'col'=2] {'row','col'}, dimensions={0}, use_global_device_ids=true | all-gather | bytes 10240 | tf_op jit(solution)/shard_map/all_gather | solution.py:24
  47.2 552.0 %while.20 = (s32[]{:T(128)}, f32[2,192,1024]{2,1,0:T(8,128)S(1)}, f32[2,192,192]{1,2,0:T(8,128)S(1)}, bf16[2048,2048]{1,0:T(8,128)(2,1)}, s32[]{:T(128)}, /*inde...) while((s32[]{:T(128)}, f32[2,192,1024]{2,1,0:T(8,128)S(1)}, ...), condition=%wide.region_7.10_spmd, body=%wide.region_4.9_spmd.sunk | while | flops 433289760 | bytes 17012348 | solution.py:122
  51.5 9.0 %all-to-all-done = bf16[4,2,16,1024]{3,2,1,0:T(8,128)(2,1)S(1)} async-done(((bf16[4,2,16,1024]{3,2,1,0:T(8,128)(2,1)}), bf16[4,2,16,1024]{3,2,1,0:T(8,128)(2,1)S(1)}, u32[]{:S(2)}, u32[]{:S(2)}) %all-to-all-start) | async-done | bytes 262176 | tf_op jit(solution)/shard_map/while/body/eval_jaxpr/all_to_all | solution.py:59
  60.6 6.0 fusion.139
  66.6 7.3 %all_to_all.62 = f32[2,2,16,1024]{3,2,1,0:T(8,128)S(1)} all-to-all(f32[2,2,16,1024]{3,2,1,0:T(8,128)S(1)} %bitcast.145), channel_id=1, replica_groups=mesh['ens'=64,'row'=2,'col'=2] {'col'}, dimensions={0} | all-to-all | bytes 524288 | tf_op jit(solution)/shard_map/while/body/eval_jaxpr/all_to_all | solution.py:19
  80.3 7.4 %all-to-all-done.2 = f32[4,1,6656]{2,1,0:T(1,128)S(1)} async-done(((f32[4,1,6656]{2,1,0:T(1,128)}), f32[4,1,6656]{2,1,0:T(1,128)S(1)}, u32[]{:S(2)}, u32[]{:S(2)}) %all-to-all-start.2) | async-done | bytes 106528 | tf_op jit(solution)/shard_map/while/body/eval_jaxpr/all_to_all | solution.py:29
  101.9 9.0 %all-to-all-done = bf16[4,2,16,1024]{3,2,1,0:T(8,128)(2,1)S(1)} async-done(((bf16[4,2,16,1024]{3,2,1,0:T(8,128)(2,1)}), bf16[4,2,16,1024]{3,2,1,0:T(8,128)(2,1)S(1)}, u32[]{:S(2)}, u32[]{:S(2)}) %all-to-all-start) | async-done | bytes 262176 | tf_op jit(solution)/shard_map/while/body/eval_jaxpr/all_to_all | solution.py:59
  111.0 6.0 fusion.139
  117.0 7.3 %all_to_all.62 = f32[2,2,16,1024]{3,2,1,0:T(8,128)S(1)} all-to-all(f32[2,2,16,1024]{3,2,1,0:T(8,128)S(1)} %bitcast.145), channel_id=1, replica_groups=mesh['ens'=64,'row'=2,'col'=2] {'col'}, dimensions={0} | all-to-all | bytes 524288 | tf_op jit(solution)/shard_map/while/body/eval_jaxpr/all_to_all | solution.py:19
  130.7 7.4 %all-to-all-done.2 = f32[4,1,6656]{2,1,0:T(1,128)S(1)} async-done(((f32[4,1,6656]{2,1,0:T(1,128)}), f32[4,1,6656]{2,1,0:T(1,128)S(1)}, u32[]{:S(2)}, u32[]{:S(2)}) %all-to-all-start.2) | async-done | bytes 106528 | tf_op jit(solution)/shard_map/while/body/eval_jaxpr/all_to_all | solution.py:29
  152.3 9.0 %all-to-all-done = bf16[4,2,16,1024]{3,2,1,0:T(8,128)(2,1)S(1)} async-done(((bf16[4,2,16,1024]{3,2,1,0:T(8,128)(2,1)}), bf16[4,2,16,1024]{3,2,1,0:T(8,128)(2,1)S(1)}, u32[]{:S(2)}, u32[]{:S(2)}) %all-to-all-start) | async-done | bytes 262176 | tf_op jit(solution)/shard_map/while/body/eval_jaxpr/all_to_all | solution.py:59
  167.3 7.3 %all_to_all.62 = f32[2,2,16,1024]{3,2,1,0:T(8,128)S(1)} all-to-all(f32[2,2,16,1024]{3,2,1,0:T(8,128)S(1)} %bitcast.145), channel_id=1, replica_groups=mesh['ens'=64,'row'=2,'col'=2] {'col'}, dimensions={0} | all-to-all | bytes 524288 | tf_op jit(solution)/shard_map/while/body/eval_jaxpr/all_to_all | solution.py:19
  181.0 7.4 %all-to-all-done.2 = f32[4,1,6656]{2,1,0:T(1,128)S(1)} async-done(((f32[4,1,6656]{2,1,0:T(1,128)}), f32[4,1,6656]{2,1,0:T(1,128)S(1)}, u32[]{:S(2)}, u32[]{:S(2)}) %all-to-all-start.2) | async-done | bytes 106528 | tf_op jit(solution)/shard_map/while/body/eval_jaxpr/all_to_all | solution.py:29
  202.6 9.0 %all-to-all-done = bf16[4,2,16,1024]{3,2,1,0:T(8,128)(2,1)S(1)} async-done(((bf16[4,2,16,1024]{3,2,1,0:T(8,128)(2,1)}), bf16[4,2,16,1024]{3,2,1,0:T(8,128)(2,1)S(1)}, u32[]{:S(2)}, u32[]{:S(2)}) %all-to-all-start) | async-done | bytes 262176 | tf_op jit(solution)/shard_map/while/body/eval_jaxpr/all_to_all | solution.py:59
  217.7 7.3 %all_to_all.62 = f32[2,2,16,1024]{3,2,1,0:T(8,128)S(1)} all-to-all(f32[2,2,16,1024]{3,2,1,0:T(8,128)S(1)} %bitcast.145), channel_id=1, replica_groups=mesh['ens'=64,'row'=2,'col'=2] {'col'}, dimensions={0} | all-to-all | bytes 524288 | tf_op jit(solution)/shard_map/while/body/eval_jaxpr/all_to_all | solution.py:19
  231.4 7.4 %all-to-all-done.2 = f32[4,1,6656]{2,1,0:T(1,128)S(1)} async-done(((f32[4,1,6656]{2,1,0:T(1,128)}), f32[4,1,6656]{2,1,0:T(1,128)S(1)}, u32[]{:S(2)}, u32[]{:S(2)}) %all-to-all-start.2) | async-done | bytes 106528 | tf_op jit(solution)/shard_map/while/body/eval_jaxpr/all_to_all | solution.py:29
  253.0 9.0 %all-to-all-done = bf16[4,2,16,1024]{3,2,1,0:T(8,128)(2,1)S(1)} async-done(((bf16[4,2,16,1024]{3,2,1,0:T(8,128)(2,1)}), bf16[4,2,16,1024]{3,2,1,0:T(8,128)(2,1)S(1)}, u32[]{:S(2)}, u32[]{:S(2)}) %all-to-all-start) | async-done | bytes 262176 | tf_op jit(solution)/shard_map/while/body/eval_jaxpr/all_to_all | solution.py:59
  262.1 6.0 fusion.139
  268.1 7.3 %all_to_all.62 = f32[2,2,16,1024]{3,2,1,0:T(8,128)S(1)} all-to-all(f32[2,2,16,1024]{3,2,1,0:T(8,128)S(1)} %bitcast.145), channel_id=1, replica_groups=mesh['ens'=64,'row'=2,'col'=2] {'col'}, dimensions={0} | all-to-all | bytes 524288 | tf_op jit(solution)/shard_map/while/body/eval_jaxpr/all_to_all | solution.py:19
  281.8 7.4 %all-to-all-done.2 = f32[4,1,6656]{2,1,0:T(1,128)S(1)} async-done(((f32[4,1,6656]{2,1,0:T(1,128)}), f32[4,1,6656]{2,1,0:T(1,128)S(1)}, u32[]{:S(2)}, u32[]{:S(2)}) %all-to-all-start.2) | async-done | bytes 106528 | tf_op jit(solution)/shard_map/while/body/eval_jaxpr/all_to_all | solution.py:29
  303.4 9.0 %all-to-all-done = bf16[4,2,16,1024]{3,2,1,0:T(8,128)(2,1)S(1)} async-done(((bf16[4,2,16,1024]{3,2,1,0:T(8,128)(2,1)}), bf16[4,2,16,1024]{3,2,1,0:T(8,128)(2,1)S(1)}, u32[]{:S(2)}, u32[]{:S(2)}) %all-to-all-start) | async-done | bytes 262176 | tf_op jit(solution)/shard_map/while/body/eval_jaxpr/all_to_all | solution.py:59
  318.4 7.3 %all_to_all.62 = f32[2,2,16,1024]{3,2,1,0:T(8,128)S(1)} all-to-all(f32[2,2,16,1024]{3,2,1,0:T(8,128)S(1)} %bitcast.145), channel_id=1, replica_groups=mesh['ens'=64,'row'=2,'col'=2] {'col'}, dimensions={0} | all-to-all | bytes 524288 | tf_op jit(solution)/shard_map/while/body/eval_jaxpr/all_to_all | solution.py:19
  332.1 7.4 %all-to-all-done.2 = f32[4,1,6656]{2,1,0:T(1,128)S(1)} async-done(((f32[4,1,6656]{2,1,0:T(1,128)}), f32[4,1,6656]{2,1,0:T(1,128)S(1)}, u32[]{:S(2)}, u32[]{:S(2)}) %all-to-all-start.2) | async-done | bytes 106528 | tf_op jit(solution)/shard_map/while/body/eval_jaxpr/all_to_all | solution.py:29
  353.7 9.0 %all-to-all-done = bf16[4,2,16,1024]{3,2,1,0:T(8,128)(2,1)S(1)} async-done(((bf16[4,2,16,1024]{3,2,1,0:T(8,128)(2,1)}), bf16[4,2,16,1024]{3,2,1,0:T(8,128)(2,1)S(1)}, u32[]{:S(2)}, u32[]{:S(2)}) %all-to-all-start) | async-done | bytes 262176 | tf_op jit(solution)/shard_map/while/body/eval_jaxpr/all_to_all | solution.py:59
  368.8 7.3 %all_to_all.62 = f32[2,2,16,1024]{3,2,1,0:T(8,128)S(1)} all-to-all(f32[2,2,16,1024]{3,2,1,0:T(8,128)S(1)} %bitcast.145), channel_id=1, replica_groups=mesh['ens'=64,'row'=2,'col'=2] {'col'}, dimensions={0} | all-to-all | bytes 524288 | tf_op jit(solution)/shard_map/while/body/eval_jaxpr/all_to_all | solution.py:19
  382.5 7.4 %all-to-all-done.2 = f32[4,1,6656]{2,1,0:T(1,128)S(1)} async-done(((f32[4,1,6656]{2,1,0:T(1,128)}), f32[4,1,6656]{2,1,0:T(1,128)S(1)}, u32[]{:S(2)}, u32[]{:S(2)}) %all-to-all-start.2) | async-done | bytes 106528 | tf_op jit(solution)/shard_map/while/body/eval_jaxpr/all_to_all | solution.py:29
  404.1 9.0 %all-to-all-done = bf16[4,2,16,1024]{3,2,1,0:T(8,128)(2,1)S(1)} async-done(((bf16[4,2,16,1024]{3,2,1,0:T(8,128)(2,1)}), bf16[4,2,16,1024]{3,2,1,0:T(8,128)(2,1)S(1)}, u32[]{:S(2)}, u32[]{:S(2)}) %all-to-all-start) | async-done | bytes 262176 | tf_op jit(solution)/shard_map/while/body/eval_jaxpr/all_to_all | solution.py:59
  413.2 6.0 fusion.139
  419.2 7.3 %all_to_all.62 = f32[2,2,16,1024]{3,2,1,0:T(8,128)S(1)} all-to-all(f32[2,2,16,1024]{3,2,1,0:T(8,128)S(1)} %bitcast.145), channel_id=1, replica_groups=mesh['ens'=64,'row'=2,'col'=2] {'col'}, dimensions={0} | all-to-all | bytes 524288 | tf_op jit(solution)/shard_map/while/body/eval_jaxpr/all_to_all | solution.py:19
  432.9 7.4 %all-to-all-done.2 = f32[4,1,6656]{2,1,0:T(1,128)S(1)} async-done(((f32[4,1,6656]{2,1,0:T(1,128)}), f32[4,1,6656]{2,1,0:T(1,128)S(1)}, u32[]{:S(2)}, u32[]{:S(2)}) %all-to-all-start.2) | async-done | bytes 106528 | tf_op jit(solution)/shard_map/while/body/eval_jaxpr/all_to_all | solution.py:29
  453.8 9.0 %all-to-all-done = bf16[4,2,16,1024]{3,2,1,0:T(8,128)(2,1)S(1)} async-done(((bf16[4,2,16,1024]{3,2,1,0:T(8,128)(2,1)}), bf16[4,2,16,1024]{3,2,1,0:T(8,128)(2,1)S(1)}, u32[]{:S(2)}, u32[]{:S(2)}) %all-to-all-start) | async-done | bytes 262176 | tf_op jit(solution)/shard_map/while/body/eval_jaxpr/all_to_all | solution.py:59
  468.8 7.3 %all_to_all.62 = f32[2,2,16,1024]{3,2,1,0:T(8,128)S(1)} all-to-all(f32[2,2,16,1024]{3,2,1,0:T(8,128)S(1)} %bitcast.145), channel_id=1, replica_groups=mesh['ens'=64,'row'=2,'col'=2] {'col'}, dimensions={0} | all-to-all | bytes 524288 | tf_op jit(solution)/shard_map/while/body/eval_jaxpr/all_to_all | solution.py:19
  482.5 7.4 %all-to-all-done.2 = f32[4,1,6656]{2,1,0:T(1,128)S(1)} async-done(((f32[4,1,6656]{2,1,0:T(1,128)}), f32[4,1,6656]{2,1,0:T(1,128)S(1)}, u32[]{:S(2)}, u32[]{:S(2)}) %all-to-all-start.2) | async-done | bytes 106528 | tf_op jit(solution)/shard_map/while/body/eval_jaxpr/all_to_all | solution.py:29
  504.0 9.0 %all-to-all-done = bf16[4,2,16,1024]{3,2,1,0:T(8,128)(2,1)S(1)} async-done(((bf16[4,2,16,1024]{3,2,1,0:T(8,128)(2,1)}), bf16[4,2,16,1024]{3,2,1,0:T(8,128)(2,1)S(1)}, u32[]{:S(2)}, u32[]{:S(2)}) %all-to-all-start) | async-done | bytes 262176 | tf_op jit(solution)/shard_map/while/body/eval_jaxpr/all_to_all | solution.py:59
  513.0 6.0 fusion.139
  519.0 7.3 %all_to_all.62 = f32[2,2,16,1024]{3,2,1,0:T(8,128)S(1)} all-to-all(f32[2,2,16,1024]{3,2,1,0:T(8,128)S(1)} %bitcast.145), channel_id=1, replica_groups=mesh['ens'=64,'row'=2,'col'=2] {'col'}, dimensions={0} | all-to-all | bytes 524288 | tf_op jit(solution)/shard_map/while/body/eval_jaxpr/all_to_all | solution.py:19
  532.7 7.4 %all-to-all-done.2 = f32[4,1,6656]{2,1,0:T(1,128)S(1)} async-done(((f32[4,1,6656]{2,1,0:T(1,128)}), f32[4,1,6656]{2,1,0:T(1,128)S(1)}, u32[]{:S(2)}, u32[]{:S(2)}) %all-to-all-start.2) | async-done | bytes 106528 | tf_op jit(solution)/shard_map/while/body/eval_jaxpr/all_to_all | solution.py:29
  554.2 9.0 %all-to-all-done = bf16[4,2,16,1024]{3,2,1,0:T(8,128)(2,1)S(1)} async-done(((bf16[4,2,16,1024]{3,2,1,0:T(8,128)(2,1)}), bf16[4,2,16,1024]{3,2,1,0:T(8,128)(2,1)S(1)}, u32[]{:S(2)}, u32[]{:S(2)}) %all-to-all-start) | async-done | bytes 262176 | tf_op jit(solution)/shard_map/while/body/eval_jaxpr/all_to_all | solution.py:59
  563.2 6.0 fusion.139
  569.3 7.3 %all_to_all.62 = f32[2,2,16,1024]{3,2,1,0:T(8,128)S(1)} all-to-all(f32[2,2,16,1024]{3,2,1,0:T(8,128)S(1)} %bitcast.145), channel_id=1, replica_groups=mesh['ens'=64,'row'=2,'col'=2] {'col'}, dimensions={0} | all-to-all | bytes 524288 | tf_op jit(solution)/shard_map/while/body/eval_jaxpr/all_to_all | solution.py:19
  582.9 7.4 %all-to-all-done.2 = f32[4,1,6656]{2,1,0:T(1,128)S(1)} async-done(((f32[4,1,6656]{2,1,0:T(1,128)}), f32[4,1,6656]{2,1,0:T(1,128)S(1)}, u32[]{:S(2)}, u32[]{:S(2)}) %all-to-all-start.2) | async-done | bytes 106528 | tf_op jit(solution)/shard_map/while/body/eval_jaxpr/all_to_all | solution.py:29
  605.7 7.7 %all-to-all-done.5 = bf16[4,2,16,1024]{3,2,1,0:T(8,128)(2,1)S(1)} async-done(((bf16[4,2,16,1024]{3,2,1,0:T(8,128)(2,1)}), bf16[4,2,16,1024]{3,2,1,0:T(8,128)(2,1)S(1)}, u32[]{:S(2)}, u32[]{:S(2)}) %all-to-all-start.5) | async-done | bytes 262176 | tf_op jit(solution)/shard_map/all_to_all | solution.py:59
  613.4 6.0 fusion.7
  619.5 7.3 %all_to_all.61 = f32[2,2,16,1024]{3,2,1,0:T(8,128)S(1)} all-to-all(f32[2,2,16,1024]{3,2,1,0:T(8,128)S(1)} %bitcast.152), channel_id=1, replica_groups=mesh['ens'=64,'row'=2,'col'=2] {'col'}, dimensions={0} | all-to-all | bytes 524288 | tf_op jit(solution)/shard_map/all_to_all | solution.py:19
  628.2 10.1 %all-gather.1 = f32[8,192,16]{1,2,0:T(8,128)S(1)} all-gather(f32[2,192,16]{1,2,0:T(8,128)S(1)} %fusion.63), channel_id=3, replica_groups=mesh['ens'=64,'row'=2,'col'=2] {'row','col'}, dimensions={0}, use_global_device_ids=true | all-gather | bytes 122880 | tf_op jit(solution)/shard_map/all_gather | solution.py:24
  (452 shorter events, 294.3 us)
Async XLA Ops:
  1.6 18.9 %all-to-all-start.3 = ((bf16[4,2,16,1024]{3,2,1,0:T(8,128)(2,1)}), bf16[4,2,16,1024]{3,2,1,0:T(8,128)(2,1)S(1)}, u32[]{:S(2)}, u32[]{:S(2)}) async-start(bf16[4,2,16,1024]{3,2,1,0:T(8,128)(2,1)} %stack.15), calls=%async_computation.3 | async-start | bytes 524288 | tf_op jit(solution)/shard_map/all_to_all | solution.py:59
  20.5 10.7 %copy-start = (f32[2,16,1024]{2,1,0:T(8,128)S(1)}, f32[2,16,1024]{2,1,0:T(8,128)}, u32[]{:S(2)}) copy-start(f32[2,16,1024]{2,1,0:T(8,128)} %param.14) | copy-start | bytes 393220
  47.2 557.7 %copy-start.2 = (s32[3]{0:T(128)S(1)}, s32[3]{0:T(128)}, u32[]{:S(2)}) copy-start(s32[3]{0:T(128)} %constant.233.clone.1) | copy-start | bytes 40
  48.0 12.5 %all-to-all-start = ((bf16[4,2,16,1024]{3,2,1,0:T(8,128)(2,1)}), bf16[4,2,16,1024]{3,2,1,0:T(8,128)(2,1)S(1)}, u32[]{:S(2)}, u32[]{:S(2)}) async-start(bf16[4,2,16,1024]{3,2,1,0:T(8,128)(2,1)} %stack.18), calls=%async_computation | async-start | bytes 524288 | tf_op jit(solution)/shard_map/while/body/eval_jaxpr/all_to_all | solution.py:59
  76.6 11.0 %all-to-all-start.2 = ((f32[4,1,6656]{2,1,0:T(1,128)}), f32[4,1,6656]{2,1,0:T(1,128)S(1)}, u32[]{:S(2)}, u32[]{:S(2)}) async-start(f32[4,1,6656]{2,1,0:T(1,128)} %broadcast_in_dim.16), calls=%async_computation.2 | async-start | bytes 212992 | tf_op jit(solution)/shard_map/while/body/eval_jaxpr/all_to_all | solution.py:29
  97.6 13.4 %all-to-all-start = ((bf16[4,2,16,1024]{3,2,1,0:T(8,128)(2,1)}), bf16[4,2,16,1024]{3,2,1,0:T(8,128)(2,1)S(1)}, u32[]{:S(2)}, u32[]{:S(2)}) async-start(bf16[4,2,16,1024]{3,2,1,0:T(8,128)(2,1)} %stack.18), calls=%async_computation | async-start | bytes 524288 | tf_op jit(solution)/shard_map/while/body/eval_jaxpr/all_to_all | solution.py:59
  127.0 11.0 %all-to-all-start.2 = ((f32[4,1,6656]{2,1,0:T(1,128)}), f32[4,1,6656]{2,1,0:T(1,128)S(1)}, u32[]{:S(2)}, u32[]{:S(2)}) async-start(f32[4,1,6656]{2,1,0:T(1,128)} %broadcast_in_dim.16), calls=%async_computation.2 | async-start | bytes 212992 | tf_op jit(solution)/shard_map/while/body/eval_jaxpr/all_to_all | solution.py:29
  147.9 13.4 %all-to-all-start = ((bf16[4,2,16,1024]{3,2,1,0:T(8,128)(2,1)}), bf16[4,2,16,1024]{3,2,1,0:T(8,128)(2,1)S(1)}, u32[]{:S(2)}, u32[]{:S(2)}) async-start(bf16[4,2,16,1024]{3,2,1,0:T(8,128)(2,1)} %stack.18), calls=%async_computation | async-start | bytes 524288 | tf_op jit(solution)/shard_map/while/body/eval_jaxpr/all_to_all | solution.py:59
  177.4 11.0 %all-to-all-start.2 = ((f32[4,1,6656]{2,1,0:T(1,128)}), f32[4,1,6656]{2,1,0:T(1,128)S(1)}, u32[]{:S(2)}, u32[]{:S(2)}) async-start(f32[4,1,6656]{2,1,0:T(1,128)} %broadcast_in_dim.16), calls=%async_computation.2 | async-start | bytes 212992 | tf_op jit(solution)/shard_map/while/body/eval_jaxpr/all_to_all | solution.py:29
  198.3 13.4 %all-to-all-start = ((bf16[4,2,16,1024]{3,2,1,0:T(8,128)(2,1)}), bf16[4,2,16,1024]{3,2,1,0:T(8,128)(2,1)S(1)}, u32[]{:S(2)}, u32[]{:S(2)}) async-start(bf16[4,2,16,1024]{3,2,1,0:T(8,128)(2,1)} %stack.18), calls=%async_computation | async-start | bytes 524288 | tf_op jit(solution)/shard_map/while/body/eval_jaxpr/all_to_all | solution.py:59
  227.7 11.0 %all-to-all-start.2 = ((f32[4,1,6656]{2,1,0:T(1,128)}), f32[4,1,6656]{2,1,0:T(1,128)S(1)}, u32[]{:S(2)}, u32[]{:S(2)}) async-start(f32[4,1,6656]{2,1,0:T(1,128)} %broadcast_in_dim.16), calls=%async_computation.2 | async-start | bytes 212992 | tf_op jit(solution)/shard_map/while/body/eval_jaxpr/all_to_all | solution.py:29
  248.7 13.4 %all-to-all-start = ((bf16[4,2,16,1024]{3,2,1,0:T(8,128)(2,1)}), bf16[4,2,16,1024]{3,2,1,0:T(8,128)(2,1)S(1)}, u32[]{:S(2)}, u32[]{:S(2)}) async-start(bf16[4,2,16,1024]{3,2,1,0:T(8,128)(2,1)} %stack.18), calls=%async_computation | async-start | bytes 524288 | tf_op jit(solution)/shard_map/while/body/eval_jaxpr/all_to_all | solution.py:59
  278.1 11.0 %all-to-all-start.2 = ((f32[4,1,6656]{2,1,0:T(1,128)}), f32[4,1,6656]{2,1,0:T(1,128)S(1)}, u32[]{:S(2)}, u32[]{:S(2)}) async-start(f32[4,1,6656]{2,1,0:T(1,128)} %broadcast_in_dim.16), calls=%async_computation.2 | async-start | bytes 212992 | tf_op jit(solution)/shard_map/while/body/eval_jaxpr/all_to_all | solution.py:29
  299.0 13.4 %all-to-all-start = ((bf16[4,2,16,1024]{3,2,1,0:T(8,128)(2,1)}), bf16[4,2,16,1024]{3,2,1,0:T(8,128)(2,1)S(1)}, u32[]{:S(2)}, u32[]{:S(2)}) async-start(bf16[4,2,16,1024]{3,2,1,0:T(8,128)(2,1)} %stack.18), calls=%async_computation | async-start | bytes 524288 | tf_op jit(solution)/shard_map/while/body/eval_jaxpr/all_to_all | solution.py:59
  328.5 11.0 %all-to-all-start.2 = ((f32[4,1,6656]{2,1,0:T(1,128)}), f32[4,1,6656]{2,1,0:T(1,128)S(1)}, u32[]{:S(2)}, u32[]{:S(2)}) async-start(f32[4,1,6656]{2,1,0:T(1,128)} %broadcast_in_dim.16), calls=%async_computation.2 | async-start | bytes 212992 | tf_op jit(solution)/shard_map/while/body/eval_jaxpr/all_to_all | solution.py:29
  349.4 13.4 %all-to-all-start = ((bf16[4,2,16,1024]{3,2,1,0:T(8,128)(2,1)}), bf16[4,2,16,1024]{3,2,1,0:T(8,128)(2,1)S(1)}, u32[]{:S(2)}, u32[]{:S(2)}) async-start(bf16[4,2,16,1024]{3,2,1,0:T(8,128)(2,1)} %stack.18), calls=%async_computation | async-start | bytes 524288 | tf_op jit(solution)/shard_map/while/body/eval_jaxpr/all_to_all | solution.py:59
  378.8 11.0 %all-to-all-start.2 = ((f32[4,1,6656]{2,1,0:T(1,128)}), f32[4,1,6656]{2,1,0:T(1,128)S(1)}, u32[]{:S(2)}, u32[]{:S(2)}) async-start(f32[4,1,6656]{2,1,0:T(1,128)} %broadcast_in_dim.16), calls=%async_computation.2 | async-start | bytes 212992 | tf_op jit(solution)/shard_map/while/body/eval_jaxpr/all_to_all | solution.py:29
  399.8 13.4 %all-to-all-start = ((bf16[4,2,16,1024]{3,2,1,0:T(8,128)(2,1)}), bf16[4,2,16,1024]{3,2,1,0:T(8,128)(2,1)S(1)}, u32[]{:S(2)}, u32[]{:S(2)}) async-start(bf16[4,2,16,1024]{3,2,1,0:T(8,128)(2,1)} %stack.18), calls=%async_computation | async-start | bytes 524288 | tf_op jit(solution)/shard_map/while/body/eval_jaxpr/all_to_all | solution.py:59
  429.2 11.0 %all-to-all-start.2 = ((f32[4,1,6656]{2,1,0:T(1,128)}), f32[4,1,6656]{2,1,0:T(1,128)S(1)}, u32[]{:S(2)}, u32[]{:S(2)}) async-start(f32[4,1,6656]{2,1,0:T(1,128)} %broadcast_in_dim.16), calls=%async_computation.2 | async-start | bytes 212992 | tf_op jit(solution)/shard_map/while/body/eval_jaxpr/all_to_all | solution.py:29
  449.4 13.4 %all-to-all-start = ((bf16[4,2,16,1024]{3,2,1,0:T(8,128)(2,1)}), bf16[4,2,16,1024]{3,2,1,0:T(8,128)(2,1)S(1)}, u32[]{:S(2)}, u32[]{:S(2)}) async-start(bf16[4,2,16,1024]{3,2,1,0:T(8,128)(2,1)} %stack.18), calls=%async_computation | async-start | bytes 524288 | tf_op jit(solution)/shard_map/while/body/eval_jaxpr/all_to_all | solution.py:59
  478.9 11.0 %all-to-all-start.2 = ((f32[4,1,6656]{2,1,0:T(1,128)}), f32[4,1,6656]{2,1,0:T(1,128)S(1)}, u32[]{:S(2)}, u32[]{:S(2)}) async-start(f32[4,1,6656]{2,1,0:T(1,128)} %broadcast_in_dim.16), calls=%async_computation.2 | async-start | bytes 212992 | tf_op jit(solution)/shard_map/while/body/eval_jaxpr/all_to_all | solution.py:29
  499.6 13.4 %all-to-all-start = ((bf16[4,2,16,1024]{3,2,1,0:T(8,128)(2,1)}), bf16[4,2,16,1024]{3,2,1,0:T(8,128)(2,1)S(1)}, u32[]{:S(2)}, u32[]{:S(2)}) async-start(bf16[4,2,16,1024]{3,2,1,0:T(8,128)(2,1)} %stack.18), calls=%async_computation | async-start | bytes 524288 | tf_op jit(solution)/shard_map/while/body/eval_jaxpr/all_to_all | solution.py:59
  529.1 11.0 %all-to-all-start.2 = ((f32[4,1,6656]{2,1,0:T(1,128)}), f32[4,1,6656]{2,1,0:T(1,128)S(1)}, u32[]{:S(2)}, u32[]{:S(2)}) async-start(f32[4,1,6656]{2,1,0:T(1,128)} %broadcast_in_dim.16), calls=%async_computation.2 | async-start | bytes 212992 | tf_op jit(solution)/shard_map/while/body/eval_jaxpr/all_to_all | solution.py:29
  549.8 13.4 %all-to-all-start = ((bf16[4,2,16,1024]{3,2,1,0:T(8,128)(2,1)}), bf16[4,2,16,1024]{3,2,1,0:T(8,128)(2,1)S(1)}, u32[]{:S(2)}, u32[]{:S(2)}) async-start(bf16[4,2,16,1024]{3,2,1,0:T(8,128)(2,1)} %stack.18), calls=%async_computation | async-start | bytes 524288 | tf_op jit(solution)/shard_map/while/body/eval_jaxpr/all_to_all | solution.py:59
  579.3 11.0 %all-to-all-start.2 = ((f32[4,1,6656]{2,1,0:T(1,128)}), f32[4,1,6656]{2,1,0:T(1,128)S(1)}, u32[]{:S(2)}, u32[]{:S(2)}) async-start(f32[4,1,6656]{2,1,0:T(1,128)} %broadcast_in_dim.16), calls=%async_computation.2 | async-start | bytes 212992 | tf_op jit(solution)/shard_map/while/body/eval_jaxpr/all_to_all | solution.py:29
  600.0 13.4 %all-to-all-start.5 = ((bf16[4,2,16,1024]{3,2,1,0:T(8,128)(2,1)}), bf16[4,2,16,1024]{3,2,1,0:T(8,128)(2,1)S(1)}, u32[]{:S(2)}, u32[]{:S(2)}) async-start(bf16[4,2,16,1024]{3,2,1,0:T(8,128)(2,1)} %stack.16), calls=%async_computation.5 | async-start | bytes 524288 | tf_op jit(solution)/shard_map/all_to_all | solution.py:59
  619.4 18.8 %copy-start.1 = (f32[2,1]{0,1:T(1,128)S(1)}, f32[2,1]{0,1:T(1,128)}, u32[]{:S(2)}) copy-start(f32[2,1]{0,1:T(1,128)} %param.16) | copy-start | bytes 28
